TPU v7x, 32 devices: a whole 2x2x4 slice. The times are simulated.
32 devices in a mesh: dom: 8 (over y, x, core), feat: 4 (over z).
Axes of the slice: x: 2, y: 2, z: 4, core: 2. Of those that a mesh axis runs over, the one named last changes fastest.
Arguments:
- features: bfloat16 [128, 131072], P('feat', 'dom'), may hold values from -6 to 6
- seed_rows: int32 [2048], P('dom'), may hold values from 0 to 16383
- want_rows: int32 [8, 8, 128], P('dom'), may hold values from 0 to 16383
- live_counts: int32 [8, 8], P('dom'), may hold values from 1 to 128, as said below
- hop_one: int32 [15, 2048], P(None, 'dom'), may hold values from 0 to 1023, as said below
- hop_two: int32 [10, 15, 2048], P(None, None, 'dom'), may hold values from 0 to 1023, as said below
- w1_self: bfloat16 [256, 128], replicated, may hold values from -0.5 to 0.5
- w1_neigh: bfloat16 [256, 128], replicated, may hold values from -0.5 to 0.5
- b1: float32 [256], P('feat'), may hold values from -4 to 4
- w2_self: bfloat16 [256, 256], P(None, 'feat'), may hold values from -0.375 to 0.375
- w2_neigh: bfloat16 [256, 256], P(None, 'feat'), may hold values from -0.375 to 0.375
- b2: float32 [256], P('feat'), may hold values from -4 to 4
Outputs:
- embed: float32 [256, 2048], P('feat', 'dom')
Inputs may be any that keep to these rules, and one draw needn't show every extreme that they name: `want_rows`: slots at or beyond live_counts[r, o] are ignored. `live_counts`: in every draw a quarter of the owners, every fourth one from a drawn offset, receive all 128 slots from every requester. `hop_one`: each entry is o * 128 + c, a position in the buffer of the requester that holds seed s, with c < live_counts of that requester and owner o. `hop_two`: each entry is o * 128 + c, a position in the buffer of the requester that holds seed s, with c < live_counts of that requester and owner o.
All inputs are finite; a program needn't handle non-finite values.
Results may differ from a plain program's by a relative error of at most 0.00036.
Values may be sent and summed in bfloat16 or wider, within the bound.
A program may use at most 64 MiB of HBM per device.

v0:
```python
import jax
import jax.numpy as jnp
from jax import lax
from jax.sharding import PartitionSpec as P

OUT = 256
FAN1 = 15
FAN2 = 10
CAP = 128


def aggregate_counts(fetched, hop_one, hop_two):
    feat_dev, slots = fetched.shape
    width = CAP * 4
    first = hop_one.reshape(1, -1)
    second = hop_two.reshape(FAN2, -1)
    columns = first.shape[1]

    def add_block(blocks, carry):
        start = blocks * width
        piece = lax.dynamic_slice_in_dim(fetched, start, width, 1)
        place = start + lax.broadcasted_iota(jnp.int32, (width, 1), 0)
        pick_one = (first == place).astype(jnp.bfloat16)
        pick_two = jnp.zeros((width, columns), jnp.bfloat16)
        for sample in range(FAN2):
            pick_two = pick_two + (second[sample : sample + 1] == place).astype(jnp.bfloat16)
        own_sum = carry[0] + jnp.dot(piece, pick_one, preferred_element_type=jnp.float32)
        mean_sum = carry[1] + jnp.dot(piece, pick_two, preferred_element_type=jnp.float32)
        return (own_sum, mean_sum)

    zeros = jnp.zeros((feat_dev, columns), jnp.float32)
    own_sum, mean_sum = lax.fori_loop(0, slots // width, add_block, (zeros, zeros))
    return (own_sum.astype(jnp.bfloat16), (mean_sum * (1.0 / FAN2)).astype(jnp.bfloat16))


def per_device(
    features,
    seed_rows,
    want_rows,
    live_counts,
    hop_one,
    hop_two,
    w1_self,
    w1_neigh,
    b1,
    w2_self,
    w2_neigh,
    b2,
):
    feat_dev = features.shape[0]
    seed_dev = seed_rows.shape[0]
    hid_dev = b1.shape[0]
    served = jnp.take(
        features,
        lax.all_to_all(want_rows, "dom", split_axis=1, concat_axis=0, tiled=True)[:, 0, :],
        axis=1,
    )
    returned = lax.all_to_all(served, "dom", split_axis=1, concat_axis=1, tiled=True)
    slot_ids = lax.broadcasted_iota(jnp.int32, (1, returned.shape[2]), 1)
    live_slots = slot_ids < live_counts[0][:, None]
    fetched = jnp.where(live_slots[None], returned, jnp.zeros((), jnp.bfloat16)).reshape(
        feat_dev, -1
    )
    x_one, m_two = aggregate_counts(fetched, hop_one, hop_two)
    x_seed = jnp.take(features, seed_rows, axis=1)
    m_one = jnp.sum(x_one.reshape(feat_dev, FAN1, seed_dev), axis=1, dtype=jnp.float32)
    m_one = (m_one * (1.0 / FAN1)).astype(jnp.bfloat16)
    selves = jnp.concatenate([x_one, x_seed], axis=1)
    means = jnp.concatenate([m_two, m_one], axis=1)
    hid_start = lax.axis_index("feat") * hid_dev
    self_rows = lax.dynamic_slice_in_dim(w1_self, hid_start, hid_dev, 0)
    neigh_rows = lax.dynamic_slice_in_dim(w1_neigh, hid_start, hid_dev, 0)
    self_part = self_rows
    neigh_part = neigh_rows
    total = jnp.dot(
        self_part,
        lax.all_gather(selves, "feat", axis=0, tiled=True),
        preferred_element_type=jnp.float32,
    )
    pre = total + jnp.dot(
        neigh_part,
        lax.all_gather(means, "feat", axis=0, tiled=True),
        preferred_element_type=jnp.float32,
    )
    hidden = jnp.maximum(pre + b1[:, None], 0.0)
    hop_cols = FAN1 * seed_dev
    h_one = hidden[:, :hop_cols]
    h_seed = hidden[:, hop_cols:]
    g_mean = jnp.sum(h_one.reshape(hid_dev, FAN1, seed_dev), axis=1) * (1.0 / FAN1)
    second_self = w2_self.astype(jnp.float32)
    second_neigh = w2_neigh.astype(jnp.float32)
    self_part = second_self
    neigh_part = second_neigh
    total = jnp.dot(
        self_part, h_seed, precision=lax.Precision.HIGHEST, preferred_element_type=jnp.float32
    )
    z_out = (
        lax.psum_scatter(
            total
            + jnp.dot(
                neigh_part,
                g_mean,
                precision=lax.Precision.HIGHEST,
                preferred_element_type=jnp.float32,
            ),
            "feat",
            scatter_dimension=0,
            tiled=True,
        )
        + b2[:, None]
    )
    square = lax.psum(jnp.sum(z_out * z_out, axis=0), "feat")
    return z_out * lax.rsqrt(square * (1.0 / OUT) + 1.0)


def solution(mesh):
    return jax.shard_map(
        per_device,
        mesh=mesh,
        in_specs=(
            P("feat", "dom"),
            P("dom"),
            P("dom", None, None),
            P("dom", None),
            P(None, "dom"),
            P(None, None, "dom"),
            P(),
            P(),
            P("feat"),
            P(None, "feat"),
            P(None, "feat"),
            P("feat"),
        ),
        out_specs=P("feat", "dom"),
        check_vma=False,
    )
```

profile of v0, /device:TPU:0, one launch (start us, length us, event | category | flops | bytes accessed | tf_op | source)
XLA Modules:
  0.0 154.3 jit_solution(16646595926999399263)
XLA Ops:
  6.5 0.0 copy-start
  6.5 0.0 copy-start.7
  6.5 0.0 copy-start.4
  6.5 0.0 copy-start.1
  6.5 5.3 %all-to-all-start = ((s32[1,8,128]{2,0,1:T(1,128)}), s32[1,8,128]{2,0,1:T(1,128)S(1)}, u32[]{:S(2)}, u32[]{:S(2)}) async-start(s32[1,8,128]{2,0,1:T(1,128)} %bitcast.38), calls=%async_computation | async-start | bytes 8192 | tf_op jit(solution)/shard_map/all_to_all | solution.py:55
  11.9 0.7 compare_select_fusion.2
  12.6 0.7 compare_and_fusion.1
  13.2 4.6 %copy.30 = bf16[32,16384]{0,1:T(8,128)(2,1)} copy(bf16[32,16384]{1,0:T(8,128)(2,1)} %param.14) | data formatting | bytes 2097152 | tf_op args[0]
  17.8 3.5 %gather_fusion.1 = bf16[256,32]{1,0:T(8,128)(2,1)S(1)} fusion(bf16[32,16384]{0,1:T(8,128)(2,1)} %copy.30, s32[1024]{0:T(1024)S(1)} %pad_clamp_fusion), kind=kCustom, calls=%fused_computation.1 | custom fusion | bytes 33792 | tf_op jit(solution)/shard_map/jit(_take)/gather | solution.py:65
  21.3 0.1 select_bitcast_fusion
  21.4 0.0 all-to-all-done
  21.4 5.6 %gather_fusion = bf16[1024,32]{1,0:T(8,128)(2,1)S(1)} fusion(bf16[32,16384]{0,1:T(8,128)(2,1)} %copy.30, s32[1024]{0:T(1024)S(1)} %fusion.43), kind=kCustom, calls=%fused_computation | custom fusion | bytes 135168 | tf_op jit(solution)/shard_map/jit(_take)/gather | solution.py:53
  27.0 0.1 copy.31
  27.2 0.6 select_bitcast_fusion.1
  27.8 4.2 %all-to-all-start.1 = ((bf16[32,8,128]{2,0,1:T(8,128)(2,1)}), bf16[32,8,128]{2,0,1:T(8,128)(2,1)S(1)}, u32[]{:S(2)}, u32[]{:S(2)}) async-start(bf16[32,8,128]{2,0,1:T(8,128)(2,1)} %select_bitcast_fusion.1), calls=%async_computation.1 | async-start | bytes 131072 | tf_op jit(solution)/shard_map/all_to_all | solution.py:58
  32.0 0.2 all-gather.3.cloned.1.call-start
  32.2 0.0 copy-done.7
  32.3 0.1 iota_compare_fusion
  32.3 0.1 copy.34
  32.4 0.0 copy-done.4
  32.4 0.0 copy-done.1
  32.5 0.1 copy.40
  32.6 4.4 %all-to-all-done.1 = bf16[32,8,128]{2,0,1:T(8,128)(2,1)S(1)} async-done(((bf16[32,8,128]{2,0,1:T(8,128)(2,1)}), bf16[32,8,128]{2,0,1:T(8,128)(2,1)S(1)}, u32[]{:S(2)}, u32[]{:S(2)}) %all-to-all-start.1) | async-done | bytes 65568 | tf_op jit(solution)/shard_map/all_to_all | solution.py:58
  37.1 19.3 %while.16 = (s32[]{:T(128)}, f32[32,3840]{1,0:T(8,128)S(1)}, f32[32,3840]{1,0:T(8,128)S(1)}, bf16[32,1024]{1,0:T(8,128)(2,1)S(1)}, s32[1,3840]{1,0:T(1,128)S(1)}...) while((s32[]{:T(128)}, f32[32,3840]{1,0:T(8,128)S(1)}, ...), condition=%wide.region_1.2_spmd.clone, body=%wide.region_0.1_spmd.clone.sunk | while | flops 311132672 | bytes 2556086 | solution.py:32
  37.1 1.5 fusion.60
  38.6 0.4 slice_reduce_fusion.11
  39.0 7.7 %convolution_add_fusion.4 = f32[32,3840]{1,0:T(8,128)S(1)} fusion(s32[3840]{0:T(1024)S(1)} %get-tuple-element.207, s32[3840]{0:T(1024)S(1)} %get-tuple-element.208, s32[3840]{0:T(1024)S(1)} %get-tuple-element.209, s32[3840]{0:T(1024)S(1)} %get-tuple-element.210, s32[3840]{0:T(1024)S(1)} %get-tuple-element.211, s32[3840]{0:T(1024)S(1)} %get-tuple-element.212, ...), kind=kOutput, calls=%fused_computation.14.clone.1 | convolution fusion | flops 183091200 | bytes 1181701 | tf_op jit(solution)/shard_map/while/body/eval_jaxpr/dot_general | solution.py:28
  46.8 1.5 fusion.60
  48.3 0.4 slice_reduce_fusion.11
  48.7 7.7 %convolution_add_fusion.4 = f32[32,3840]{1,0:T(8,128)S(1)} fusion(s32[3840]{0:T(1024)S(1)} %get-tuple-element.207, s32[3840]{0:T(1024)S(1)} %get-tuple-element.208, s32[3840]{0:T(1024)S(1)} %get-tuple-element.209, s32[3840]{0:T(1024)S(1)} %get-tuple-element.210, s32[3840]{0:T(1024)S(1)} %get-tuple-element.211, s32[3840]{0:T(1024)S(1)} %get-tuple-element.212, ...), kind=kOutput, calls=%fused_computation.14.clone.1 | convolution fusion | flops 183091200 | bytes 1181701 | tf_op jit(solution)/shard_map/while/body/eval_jaxpr/dot_general | solution.py:28
  56.4 0.0 copy-start.6
  56.5 0.2 reshape.90
  56.7 0.7 pad_maximum_fusion
  57.4 0.0 all-gather.3.cloned.1.call-update
  57.4 0.0 all-gather.5.cloned.1.call-start
  57.5 0.1 reduce_sum.27
  57.6 0.0 copy-start.3
  57.7 0.7 pad_maximum_fusion.1
  58.4 0.0 all-gather.5.cloned.1.call-update
  58.4 0.0 reduce-scatter.4.cloned.1.call-start
  58.5 26.5 %all-gather.3.cloned.1.call-done = bf16[128,4096]{1,0:T(8,128)(2,1)} async-done(((bf16[32,4096]{1,0:T(8,128)(2,1)}), bf16[128,4096]{1,0:T(8,128)(2,1)}) %all-gather.3.cloned.1.call-update) | async-done | bytes 1048592 | tf_op jit(solution)/shard_map/all_gather | solution.py:77
  84.9 0.0 copy-done
  84.9 1.5 fusion.40
  86.4 0.0 copy-start.2
  86.5 27.4 %all-gather.5.cloned.1.call-done = bf16[128,4096]{1,0:T(8,128)(2,1)} async-done(((bf16[32,4096]{1,0:T(8,128)(2,1)}), bf16[128,4096]{1,0:T(8,128)(2,1)}) %all-gather.5.cloned.1.call-update) | async-done | bytes 1048592 | tf_op jit(solution)/shard_map/all_gather | solution.py:82
  113.9 0.0 copy-done.6
  113.9 1.5 fusion.33
  115.4 0.0 copy-start.5
  115.4 0.1 slice.93
  115.5 0.0 copy-done.3
  115.5 0.3 fusion.35
  115.9 0.3 reshape.89
  116.2 0.2 reduce_sum.28
  116.4 0.0 copy-done.2
  116.4 0.3 fusion.34
  116.7 0.8 copy.36
  117.5 0.0 reduce-scatter.4.cloned.1.call-update
  117.5 19.5 %reduce-scatter.4.cloned.1.call-done = f32[64,256]{1,0:T(8,128)} async-done(((f32[256,256]{1,0:T(8,128)}), f32[64,256]{1,0:T(8,128)}) %reduce-scatter.4.cloned.1.call-update) | async-done | bytes 65552
  137.1 0.9 copy.37
  138.0 0.0 copy-done.5
  138.0 0.1 multiply_reduce_fusion
  138.1 8.8 %psum.7 = f32[256]{0:T(256)S(1)} all-reduce(f32[256]{0:T(256)S(1)} %multiply_reduce_fusion), channel_id=1, replica_groups=mesh['dom'=8,'feat'=4] {'feat'}, use_global_device_ids=true, to_apply=%region_6.7 | all-reduce | flops 256 | bytes 2048 | tf_op jit(solution)/shard_map/psum | solution.py:112
  147.0 0.1 add_multiply_fusion
  147.1 0.7 copy.35
  (16 shorter events, 0.2 us)
Async XLA Ops:
  6.5 78.4 %copy-start = (bf16[256,128]{1,0:T(8,128)(2,1)S(1)}, bf16[256,128]{1,0:T(8,128)(2,1)}, u32[]{:S(2)}) copy-start(bf16[256,128]{1,0:T(8,128)(2,1)} %param.20) | copy-start | bytes 196612
  6.5 25.7 %copy-start.7 = (s32[1,8]{1,0:T(1,128)S(1)}, s32[1,8]{1,0:T(1,128)}, u32[]{:S(2)}) copy-start(s32[1,8]{1,0:T(1,128)} %param.17) | copy-start | bytes 100
  6.5 25.9 %copy-start.4 = (s32[15,256]{1,0:T(8,128)S(1)}, s32[15,256]{1,0:T(8,128)}, u32[]{:S(2)}) copy-start(s32[15,256]{1,0:T(8,128)} %param.18) | copy-start | bytes 46084
  6.5 25.9 %copy-start.1 = (s32[10,15,256]{2,1,0:T(8,128)S(1)}, s32[10,15,256]{2,1,0:T(8,128)}, u32[]{:S(2)}) copy-start(s32[10,15,256]{2,1,0:T(8,128)} %param.19) | copy-start | bytes 460804
  6.5 14.9 %all-to-all-start = ((s32[1,8,128]{2,0,1:T(1,128)}), s32[1,8,128]{2,0,1:T(1,128)S(1)}, u32[]{:S(2)}, u32[]{:S(2)}) async-start(s32[1,8,128]{2,0,1:T(1,128)} %bitcast.38), calls=%async_computation | async-start | bytes 8192 | tf_op jit(solution)/shard_map/all_to_all | solution.py:55
  27.8 9.2 %all-to-all-start.1 = ((bf16[32,8,128]{2,0,1:T(8,128)(2,1)}), bf16[32,8,128]{2,0,1:T(8,128)(2,1)S(1)}, u32[]{:S(2)}, u32[]{:S(2)}) async-start(bf16[32,8,128]{2,0,1:T(8,128)(2,1)} %select_bitcast_fusion.1), calls=%async_computation.1 | async-start | bytes 131072 | tf_op jit(solution)/shard_map/all_to_all | solution.py:58
  32.0 52.9 %all-gather.3.cloned.1.call-start = ((), (), s32[]{:S(2)}) async-start(), calls=%async_computation.3 | async-start | bytes 1310720 | tf_op jit(solution)/shard_map/all_gather | solution.py:77
  56.4 57.5 %copy-start.6 = (f32[64]{0:T(128)S(1)}, f32[64]{0:T(128)}, u32[]{:S(2)}) copy-start(f32[64]{0:T(128)} %param.22) | copy-start | bytes 772
  57.4 56.5 %all-gather.5.cloned.1.call-start = ((), (), s32[]{:S(2)}) async-start(), calls=%async_computation.4 | async-start | bytes 1310720 | tf_op jit(solution)/shard_map/all_gather | solution.py:82
  57.6 57.9 %copy-start.3 = (bf16[256,64]{0,1:T(8,128)(2,1)S(1)}, bf16[256,64]{0,1:T(8,128)(2,1)}, u32[]{:S(2)}) copy-start(bf16[256,64]{0,1:T(8,128)(2,1)} %param.23) | copy-start | bytes 98308
  58.4 78.7 %reduce-scatter.4.cloned.1.call-start = ((), (), s32[]{:S(2)}) async-start(), calls=%async_computation.5 | async-start | bytes 327680
  86.4 29.9 %copy-start.2 = (bf16[256,64]{0,1:T(8,128)(2,1)S(1)}, bf16[256,64]{0,1:T(8,128)(2,1)}, u32[]{:S(2)}) copy-start(bf16[256,64]{0,1:T(8,128)(2,1)} %param.24) | copy-start | bytes 98308
  115.4 22.6 %copy-start.5 = (f32[64]{0:T(128)S(1)}, f32[64]{0:T(128)}, u32[]{:S(2)}) copy-start(f32[64]{0:T(128)} %param.25) | copy-start | bytes 772
Sparse Core Ops, SparseCore 0:
  57.5 27.3 all-gather.2
  86.5 27.3 all-gather.4
  117.7 19.3 reduce-scatter.3
where the time goes:
time: 155 us; the launch traced here: 154 us
  waiting for transfers between devices  77.9 us (50%)
  matrix products  22 us (14%)
  local copies, waits for them, and re-layouts  17.9 us (12%)
  between operations  13.4 us (9%)
  starting transfers between devices  9.84 us (6%)
  blocking collectives  8.85 us (6%)
  other arithmetic  4.35 us (3%)
    all_gather x1, waiting for transfers between devices, per_device(): lax.all_gather(means, 'feat', axis=0, tiled=True)  27.4 us
    all_gather x1, waiting for transfers between devices, per_device(): lax.all_gather(selves, 'feat', axis=0, tiled=True)  26.5 us
    unnamed x4, waiting for transfers between devices  19.6 us
    dot_general x2, matrix products, add_block(): jnp.dot(piece, pick_two, preferred_element_type=jnp.float32)  15.4 us
    psum x1, blocking collectives, per_device(): square = lax.psum(jnp.sum(z_out * z_out, axis=0), 'feat')  8.85 us
    unnamed x22, local copies, waits for them, and re-layouts  6.56 us
    gather x2, local copies, waits for them, and re-layouts, per_device(): jnp.take(features, lax.all_to_all(want_rows, 'dom', split_axis=1, concat_...  5.73 us
    all_to_all x1, starting transfers between devices, per_device(): lax.all_to_all(want_rows, 'dom', split_axis=1, concat_axis=0, tiled=True)  5.34 us
  transfers between devices with their start and end apart: 5, of which 4 were waited for; matrix products, arithmetic and copies ran while one was open for 8% of the time, Pallas kernels for 0%

commit v1 on v0

--- a/solution.py
+++ b/solution.py
@@ -55,7 +55,10 @@
         lax.all_to_all(want_rows, "dom", split_axis=1, concat_axis=0, tiled=True)[:, 0, :],
         axis=1,
     )
-    returned = lax.all_to_all(served, "dom", split_axis=1, concat_axis=1, tiled=True)
+    returned = jnp.concatenate(
+        lax.all_to_all(jnp.stack(jnp.split(served, lax.axis_size("dom"), axis=1)), "dom", 0, 0),
+        axis=1,
+    )
     slot_ids = lax.broadcasted_iota(jnp.int32, (1, returned.shape[2]), 1)
     live_slots = slot_ids < live_counts[0][:, None]
     fetched = jnp.where(live_slots[None], returned, jnp.zeros((), jnp.bfloat16)).reshape(

time: 155 us -> 160 us (1.032)
  local copies, waits for them, and re-layouts: 17.9 us -> 23.4 us
    unnamed x22 -> x27, local copies, waits for them, and re-layouts: 6.56 us -> 10.7 us
  transfers between devices with their start and end apart: 5 -> 5, of which waited for: 4 -> 4; matrix products, arithmetic and copies ran while one was open for 8% -> 6% of each run, Pallas kernels for 0% -> 0%
where the time goes in v1:
time: 160 us; the launch traced here: 159 us
  waiting for transfers between devices  78.1 us (49%)
  local copies, waits for them, and re-layouts  23.4 us (15%)
  matrix products  22 us (14%)
  between operations  13.4 us (8%)
  starting transfers between devices  9.83 us (6%)
  blocking collectives  8.75 us (5%)
  other arithmetic  3.66 us (2%)
    all_gather x1, waiting for transfers between devices, per_device(): lax.all_gather(means, 'feat', axis=0, tiled=True)  27.4 us
    all_gather x1, waiting for transfers between devices, per_device(): lax.all_gather(selves, 'feat', axis=0, tiled=True)  26.5 us
    unnamed x4, waiting for transfers between devices  19.6 us
    dot_general x2, matrix products, add_block(): jnp.dot(piece, pick_two, preferred_element_type=jnp.float32)  15.4 us
    unnamed x27, local copies, waits for them, and re-layouts  10.7 us
    psum x1, blocking collectives, per_device(): square = lax.psum(jnp.sum(z_out * z_out, axis=0), 'feat')  8.75 us
    gather x2, local copies, waits for them, and re-layouts, per_device(): jnp.take(features, lax.all_to_all(want_rows, 'dom', split_axis=1, concat_...  5.73 us
    all_to_all x1, starting transfers between devices, per_device(): lax.all_to_all(want_rows, 'dom', split_axis=1, concat_axis=0, tiled=True)  5.33 us
  transfers between devices with their start and end apart: 5, of which 4 were waited for; matrix products, arithmetic and copies ran while one was open for 6% of the time, Pallas kernels for 0%

profile of v1, /device:TPU:0, one launch (start us, length us, event | category | flops | bytes accessed | tf_op | source)
XLA Modules:
  0.0 159.3 jit_solution(15556391468556259631)
XLA Ops:
  6.5 0.0 copy-start
  6.5 5.3 %all-to-all-start = ((s32[1,8,128]{2,0,1:T(1,128)}), s32[1,8,128]{2,0,1:T(1,128)S(1)}, u32[]{:S(2)}, u32[]{:S(2)}) async-start(s32[1,8,128]{2,0,1:T(1,128)} %bitcast.77), calls=%async_computation | async-start | bytes 8192 | tf_op jit(solution)/shard_map/all_to_all | solution.py:55
  11.9 0.7 compare_select_fusion.2
  12.6 0.7 lt.69
  13.3 0.7 compare_and_fusion.1
  14.0 4.6 %copy.30 = bf16[32,16384]{0,1:T(8,128)(2,1)} copy(bf16[32,16384]{1,0:T(8,128)(2,1)} %param.14) | data formatting | bytes 2097152 | tf_op args[0]
  18.6 0.0 copy-done.4
  18.6 0.0 copy-done.1
  18.6 0.1 copy.40
  18.8 0.0 all-to-all-done
  18.8 3.5 %gather_fusion.1 = bf16[256,32]{1,0:T(8,128)(2,1)S(1)} fusion(bf16[32,16384]{0,1:T(8,128)(2,1)} %copy.30, s32[1024]{0:T(1024)S(1)} %get-tuple-element.161), kind=kCustom, calls=%fused_computation.1 | custom fusion | bytes 33792 | tf_op jit(solution)/shard_map/jit(_take)/gather | solution.py:68
  22.3 5.6 %gather_fusion = bf16[1024,32]{1,0:T(8,128)(2,1)S(1)} fusion(bf16[32,16384]{0,1:T(8,128)(2,1)} %copy.30, s32[1024]{0:T(1024)S(1)} %get-tuple-element.160), kind=kCustom, calls=%fused_computation | custom fusion | bytes 135168 | tf_op jit(solution)/shard_map/jit(_take)/gather | solution.py:53
  27.9 0.1 copy.31
  28.0 0.6 constant_dynamic-update-slice_fusion.7
  28.6 0.6 constant_dynamic-update-slice_fusion.6
  29.2 0.6 constant_dynamic-update-slice_fusion.5
  29.8 0.6 constant_dynamic-update-slice_fusion.4
  30.4 0.6 constant_dynamic-update-slice_fusion.3
  31.0 0.6 constant_dynamic-update-slice_fusion.2
  31.6 0.6 constant_dynamic-update-slice_fusion.1
  32.2 0.6 constant_dynamic-update-slice_fusion
  32.8 4.2 %all-to-all-start.1 = ((bf16[8,32,1,128]{3,1,2,0:T(8,128)(2,1)}), bf16[8,32,1,128]{3,1,2,0:T(8,128)(2,1)S(1)}, u32[]{:S(2)}, u32[]{:S(2)}) async-start(bf16[8,32,1,128]{3,1,2,0:T(8,128)(2,1)} %constant_dynamic-update-slice_fusion), calls=%async_computation.1 | async-start | bytes 131072 | tf_op jit(solution)/shard_map/all_to_all | solution.py:59
  37.0 0.2 all-gather.3.cloned.1.call-start
  37.3 0.1 select_bitcast_fusion
  37.4 0.1 copy.34
  37.4 4.6 %all-to-all-done.1 = bf16[8,32,1,128]{3,1,2,0:T(8,128)(2,1)S(1)} async-done(((bf16[8,32,1,128]{3,1,2,0:T(8,128)(2,1)}), bf16[8,32,1,128]{3,1,2,0:T(8,128)(2,1)S(1)}, u32[]{:S(2)}, u32[]{:S(2)}) %all-to-all-start.1) | async-done | bytes 65568 | tf_op jit(solution)/shard_map/all_to_all | solution.py:59
  42.1 19.3 %while.16 = (s32[]{:T(128)}, f32[32,3840]{1,0:T(8,128)S(1)}, f32[32,3840]{1,0:T(8,128)S(1)}, bf16[32,1024]{1,0:T(8,128)(2,1)S(1)}, s32[1,3840]{1,0:T(1,128)S(1)}...) while((s32[]{:T(128)}, f32[32,3840]{1,0:T(8,128)S(1)}, ...), condition=%wide.region_1.2_spmd.clone, body=%wide.region_0.1_spmd.clone.sunk | while | flops 311132672 | bytes 2556086 | solution.py:32
  42.2 1.5 fusion.60
  43.7 0.4 slice_reduce_fusion.11
  44.1 7.7 %convolution_add_fusion.4 = f32[32,3840]{1,0:T(8,128)S(1)} fusion(s32[3840]{0:T(1024)S(1)} %get-tuple-element.209, s32[3840]{0:T(1024)S(1)} %get-tuple-element.210, s32[3840]{0:T(1024)S(1)} %get-tuple-element.211, s32[3840]{0:T(1024)S(1)} %get-tuple-element.212, s32[3840]{0:T(1024)S(1)} %get-tuple-element.213, s32[3840]{0:T(1024)S(1)} %get-tuple-element.214, ...), kind=kOutput, calls=%fused_computation.14.clone.1 | convolution fusion | flops 183091200 | bytes 1181701 | tf_op jit(solution)/shard_map/while/body/eval_jaxpr/dot_general | solution.py:28
  51.9 1.5 fusion.60
  53.3 0.4 slice_reduce_fusion.11
  53.7 7.7 %convolution_add_fusion.4 = f32[32,3840]{1,0:T(8,128)S(1)} fusion(s32[3840]{0:T(1024)S(1)} %get-tuple-element.209, s32[3840]{0:T(1024)S(1)} %get-tuple-element.210, s32[3840]{0:T(1024)S(1)} %get-tuple-element.211, s32[3840]{0:T(1024)S(1)} %get-tuple-element.212, s32[3840]{0:T(1024)S(1)} %get-tuple-element.213, s32[3840]{0:T(1024)S(1)} %get-tuple-element.214, ...), kind=kOutput, calls=%fused_computation.14.clone.1 | convolution fusion | flops 183091200 | bytes 1181701 | tf_op jit(solution)/shard_map/while/body/eval_jaxpr/dot_general | solution.py:28
  61.5 0.0 copy-start.6
  61.5 0.2 reshape.98
  61.7 0.7 pad_maximum_fusion
  62.5 0.0 all-gather.3.cloned.1.call-update
  62.5 0.0 all-gather.5.cloned.1.call-start
  62.5 0.1 reduce_sum.27
  62.7 0.0 copy-start.3
  62.7 0.7 pad_maximum_fusion.1
  63.4 0.0 all-gather.5.cloned.1.call-update
  63.4 0.0 reduce-scatter.4.cloned.1.call-start
  63.5 26.5 %all-gather.3.cloned.1.call-done = bf16[128,4096]{1,0:T(8,128)(2,1)} async-done(((bf16[32,4096]{1,0:T(8,128)(2,1)}), bf16[128,4096]{1,0:T(8,128)(2,1)}) %all-gather.3.cloned.1.call-update) | async-done | bytes 1048592 | tf_op jit(solution)/shard_map/all_gather | solution.py:80
  90.0 0.0 copy-done
  90.0 1.5 fusion.40
  91.5 0.0 copy-start.2
  91.5 27.4 %all-gather.5.cloned.1.call-done = bf16[128,4096]{1,0:T(8,128)(2,1)} async-done(((bf16[32,4096]{1,0:T(8,128)(2,1)}), bf16[128,4096]{1,0:T(8,128)(2,1)}) %all-gather.5.cloned.1.call-update) | async-done | bytes 1048592 | tf_op jit(solution)/shard_map/all_gather | solution.py:85
  118.9 1.5 fusion.33
  120.5 0.0 copy-start.5
  120.5 0.1 slice.93
  120.6 0.0 copy-done.3
  120.6 0.3 fusion.35
  120.9 0.3 reshape.97
  121.2 0.2 reduce_sum.28
  121.4 0.3 fusion.34
  121.7 0.8 copy.36
  122.6 0.0 reduce-scatter.4.cloned.1.call-update
  122.6 19.5 %reduce-scatter.4.cloned.1.call-done = f32[64,256]{1,0:T(8,128)} async-done(((f32[256,256]{1,0:T(8,128)}), f32[64,256]{1,0:T(8,128)}) %reduce-scatter.4.cloned.1.call-update) | async-done | bytes 65552
  142.1 0.9 copy.37
  143.1 0.1 multiply_reduce_fusion
  143.2 8.8 %psum.7 = f32[256]{0:T(256)S(1)} all-reduce(f32[256]{0:T(256)S(1)} %multiply_reduce_fusion), channel_id=1, replica_groups=mesh['dom'=8,'feat'=4] {'feat'}, use_global_device_ids=true, to_apply=%region_6.7 | all-reduce | flops 256 | bytes 2048 | tf_op jit(solution)/shard_map/psum | solution.py:115
  151.9 0.1 add_multiply_fusion
  152.0 0.7 copy.35
  (23 shorter events, 0.3 us)
Async XLA Ops:
  6.5 83.4 %copy-start = (bf16[256,128]{1,0:T(8,128)(2,1)S(1)}, bf16[256,128]{1,0:T(8,128)(2,1)}, u32[]{:S(2)}) copy-start(bf16[256,128]{1,0:T(8,128)(2,1)} %param.20) | copy-start | bytes 196612
  6.5 12.0 %copy-start.4 = (s32[15,256]{1,0:T(8,128)S(1)}, s32[15,256]{1,0:T(8,128)}, u32[]{:S(2)}) copy-start(s32[15,256]{1,0:T(8,128)} %param.18) | copy-start | bytes 46084
  6.5 12.0 %copy-start.1 = (s32[10,15,256]{2,1,0:T(8,128)S(1)}, s32[10,15,256]{2,1,0:T(8,128)}, u32[]{:S(2)}) copy-start(s32[10,15,256]{2,1,0:T(8,128)} %param.19) | copy-start | bytes 460804
  6.5 12.2 %all-to-all-start = ((s32[1,8,128]{2,0,1:T(1,128)}), s32[1,8,128]{2,0,1:T(1,128)S(1)}, u32[]{:S(2)}, u32[]{:S(2)}) async-start(s32[1,8,128]{2,0,1:T(1,128)} %bitcast.77), calls=%async_computation | async-start | bytes 8192 | tf_op jit(solution)/shard_map/all_to_all | solution.py:55
  32.8 9.2 %all-to-all-start.1 = ((bf16[8,32,1,128]{3,1,2,0:T(8,128)(2,1)}), bf16[8,32,1,128]{3,1,2,0:T(8,128)(2,1)S(1)}, u32[]{:S(2)}, u32[]{:S(2)}) async-start(bf16[8,32,1,128]{3,1,2,0:T(8,128)(2,1)} %constant_dynamic-update-slice_fusion), calls=%async_computation.1 | async-start | bytes 131072 | tf_op jit(solution)/shard_map/all_to_all | solution.py:59
  37.0 52.9 %all-gather.3.cloned.1.call-start = ((), (), s32[]{:S(2)}) async-start(), calls=%async_computation.3 | async-start | bytes 1310720 | tf_op jit(solution)/shard_map/all_gather | solution.py:80
  61.5 57.5 %copy-start.6 = (f32[64]{0:T(128)S(1)}, f32[64]{0:T(128)}, u32[]{:S(2)}) copy-start(f32[64]{0:T(128)} %param.22) | copy-start | bytes 772
  62.5 56.5 %all-gather.5.cloned.1.call-start = ((), (), s32[]{:S(2)}) async-start(), calls=%async_computation.4 | async-start | bytes 1310720 | tf_op jit(solution)/shard_map/all_gather | solution.py:85
  62.7 57.9 %copy-start.3 = (bf16[256,64]{0,1:T(8,128)(2,1)S(1)}, bf16[256,64]{0,1:T(8,128)(2,1)}, u32[]{:S(2)}) copy-start(bf16[256,64]{0,1:T(8,128)(2,1)} %param.23) | copy-start | bytes 98308
  63.4 78.7 %reduce-scatter.4.cloned.1.call-start = ((), (), s32[]{:S(2)}) async-start(), calls=%async_computation.5 | async-start | bytes 327680
  91.5 29.9 %copy-start.2 = (bf16[256,64]{0,1:T(8,128)(2,1)S(1)}, bf16[256,64]{0,1:T(8,128)(2,1)}, u32[]{:S(2)}) copy-start(bf16[256,64]{0,1:T(8,128)(2,1)} %param.24) | copy-start | bytes 98308
  120.5 22.6 %copy-start.5 = (f32[64]{0:T(128)S(1)}, f32[64]{0:T(128)}, u32[]{:S(2)}) copy-start(f32[64]{0:T(128)} %param.25) | copy-start | bytes 772
Sparse Core Ops, SparseCore 0:
  62.6 27.3 all-gather.2
  91.5 27.3 all-gather.4
  122.7 19.3 reduce-scatter.3
